TPU v7x, 32 devices: a whole 2x2x4 slice. The times are simulated.
32 devices in a mesh: leaf: 32 (over z, y, x, core).
Axes of the slice: x: 2, y: 2, z: 4, core: 2. Of those that a mesh axis runs over, the one named last changes fastest.
Arguments:
- leaf_inverses: float32 [32768, 1024], P('leaf'), may hold values from -1 to 1, as said below
- u_bases: float32 [32768, 320], P('leaf'), may hold values from -6 to 6
- v_bases: float32 [32768, 320], P('leaf'), may hold values from -6 to 6
- right_side: float32 [32768, 128], P('leaf'), may hold values from -6 to 6
Outputs:
- solution: float32 [32768, 128], P('leaf')
Inputs may be any that keep to these rules, and one draw needn't show every extreme that they name: `leaf_inverses`: every run of 1024 rows starting at a multiple of 1024 is the inverse of a symmetric positive definite 1024 x 1024 matrix.
All inputs are finite; a program needn't handle non-finite values.
Results may differ from a plain program's by a relative error of at most 0.00014.
Values sent between devices are 32-bit elements; how exact they have to be, the bound alone decides.
A program may use at most 64 MiB of HBM per device.

v0:
```python
import jax
import jax.numpy as jnp
import numpy as np
from jax import lax
from jax.sharding import PartitionSpec as P

RANK = 64


PRECISE = lax.Precision.HIGHEST


def swapped(block, axis, bit):
    count = lax.axis_size(axis)
    route = []
    for low in range(count):
        high = low | 1 << bit
        if high != low and high < count:
            route += [(low, high), (high, low)]
    return lax.ppermute(block, axis, route)


def matmul(left, right):
    return jnp.dot(left, right, precision=PRECISE, preferred_element_type=jnp.float32)


def inner_rows(left, right):
    return lax.dot_general(
        left, right, (((0,), (0,)), ((), ())), precision=PRECISE, preferred_element_type=jnp.float32
    )


def cholesky_solve(block, right_cols):
    factor = jnp.linalg.cholesky(block)
    partial_value = lax.linalg.triangular_solve(factor, right_cols, left_side=True, lower=True)
    return lax.linalg.triangular_solve(
        factor, partial_value, left_side=True, lower=True, transpose_a=True
    )


def couple(lower_gram, upper_gram):
    across_up = upper_gram[:, :RANK]
    across_low = lower_gram[:, :RANK]
    right_up = upper_gram[:, RANK:]
    right_low = lower_gram[:, RANK:]
    schur_block = jnp.eye(RANK, dtype=jnp.float32) - matmul(across_low, across_up)
    target = right_low - matmul(across_low, right_up)
    high_coef = cholesky_solve(matmul(schur_block.T, schur_block), matmul(schur_block.T, target))
    low_coef = right_up - matmul(across_up, high_coef)
    return (low_coef, high_coef)


def body(leaf_inverses, u_bases, v_bases, right_side):
    leaf_size = leaf_inverses.shape[0]
    levels = lax.axis_size("leaf").bit_length() - 1
    scales = np.repeat(2.0 / (leaf_size * 2.0 ** np.arange(levels)), RANK).astype(np.float32)
    carried = matmul(leaf_inverses, jnp.concatenate([u_bases * scales, right_side], 1))
    position = lax.axis_index("leaf")
    grams_own = inner_rows(v_bases, carried)
    for height in range(1, levels + 1):
        grams_sib = swapped(grams_own, "leaf", height - 1)
        is_upper = position // 2 ** (height - 1) % 2 == 1
        lower_gram = jnp.where(is_upper, grams_sib, grams_own)
        upper_gram = jnp.where(is_upper, grams_own, grams_sib)
        low_coef, high_coef = couple(lower_gram[:RANK], upper_gram[:RANK])
        carried = carried[:, RANK:] - matmul(
            carried[:, :RANK], jnp.where(is_upper, high_coef, low_coef)
        )
        lower_next = lower_gram[RANK:, RANK:] - matmul(lower_gram[RANK:, :RANK], low_coef)
        upper_next = upper_gram[RANK:, RANK:] - matmul(upper_gram[RANK:, :RANK], high_coef)
        grams_own = lower_next + upper_next
    return carried


def solution(mesh):
    in_specs = (P("leaf", None), P("leaf", None), P("leaf", None), P("leaf", None))
    out_specs = P("leaf", None)
    return jax.shard_map(body, mesh=mesh, in_specs=in_specs, out_specs=out_specs, check_vma=False)
```

profile of v0, /device:TPU:0, one launch (start us, length us, event | category | flops | bytes accessed | tf_op | source)
XLA Modules:
  0.0 130.0 jit_solution(6447961077742954046)
XLA Ops:
  0.0 2.1 %copy.6 = f32[1024,128]{0,1:T(8,128)} copy(f32[1024,128]{1,0:T(8,128)} %param.9) | data formatting | bytes 1048576 | tf_op args[3]
  3.7 8.4 %fusion = f32[448,1024]{1,0:T(8,128)S(1)} fusion(f32[1024,1024]{1,0:T(8,128)} %param.6, f32[1024,128]{0,1:T(8,128)S(1)} %copy-done.3, f32[1024,320]{0,1:T(8,128)S(1)} %broadcast_multiply_fusion), kind=kOutput, calls=%fused_computation | convolution fusion | flops 5637603328 | bytes 7864320 | tf_op jit(solution)/shard_map/dot_general | solution.py:24
  12.1 3.1 %convolution_bitcast_fusion = f32[320,448]{1,0:T(8,128)} fusion(f32[448,1024]{1,0:T(8,128)S(1)} %fusion, f32[1024,320]{0,1:T(8,128)S(1)} %copy-done), kind=kOutput, calls=%fused_computation.8 | convolution fusion | flops 1761607680 | bytes 3719168 | tf_op jit(solution)/shard_map/dot_general | solution.py:28
  15.7 2.1 %collective-permute-done = f32[320,448]{1,0:T(8,128)} collective-permute-done((f32[320,448]{1,0:T(8,128)}, f32[320,448]{1,0:T(8,128)}, u32[]{:S(2)}, u32[]{:S(2)}) %collective-permute-start) | collective-permute-done | bytes 573472 | tf_op jit(solution)/shard_map/ppermute | solution.py:20
  21.1 5.8 %cholesky.89 = f32[64,64]{1,0:T(8,128)S(1)} custom-call(f32[64,64]{1,0:T(8,128)S(1)} %fusion.86), custom_call_target="Cholesky" | custom-call | tf_op jit(solution)/shard_map/jit(cholesky)/cholesky | solution.py:34
  28.2 4.9 %custom-call.27 = f32[1,64,64]{1,2,0:T(8,128)S(1)} custom-call(f32[1,64,64]{2,1,0:T(8,128)S(1)} %fusion.50), custom_call_target="InvertDiagBlocksLowerTriangular" | custom-call | tf_op jit(solution)/shard_map/triangular_solve | solution.py:36
  36.3 2.4 %fusion.5 = f32[256,384]{1,0:T(8,128)} fusion(f32[320,448]{1,0:T(8,128)} %copy-done.4, f32[256,384]{1,0:T(8,128)S(1)} %fusion.17, f32[320,448]{1,0:T(8,128)S(1)} %copy-done.2, f32[64,384]{1,0:T(8,128)S(1)} %fusion.82), kind=kOutput, calls=%fused_computation.23 | convolution fusion | flops 75792384 | bytes 1802240 | tf_op jit(solution)/shard_map/dot_general | solution.py:24
  38.6 2.8 %collective-permute-start.1 = (f32[256,384]{1,0:T(8,128)}, f32[256,384]{1,0:T(8,128)}, u32[]{:S(2)}, u32[]{:S(2)}) collective-permute-start(f32[256,384]{1,0:T(8,128)} %fusion.5), channel_id=1, source_target_pairs={{0,2},{2,0},{1,3},{3,1},{4,6},{6,4},{5,7},{7,5},{8,10},{10,8},{9,1... | collective-permute-start | bytes 1179656 | tf_op jit(solution)/shard_map/ppermute | solution.py:20
  41.5 2.6 %slice_subtract_fusion = f32[1024,384]{0,1:T(8,128)} fusion(f32[1024,448]{0,1:T(8,128)S(1)} %bitcast.100, f32[64,384]{1,0:T(8,128)S(1)} %fusion.82, f32[64,384]{1,0:T(8,128)S(1)} %convolution_subtract_fusion.5, pred[]{:T(512)S(6)} %eq.36), kind=kOutput, calls=%fused_computation.4 | convolution fusion | flops 302407680 | bytes 3604481 | tf_op jit(solution)/shard_map/dot_general | solution.py:24
  44.1 7.1 %collective-permute-done.1 = f32[256,384]{1,0:T(8,128)} collective-permute-done((f32[256,384]{1,0:T(8,128)}, f32[256,384]{1,0:T(8,128)}, u32[]{:S(2)}, u32[]{:S(2)}) %collective-permute-start.1) | collective-permute-done | bytes 393248 | tf_op jit(solution)/shard_map/ppermute | solution.py:20
  53.5 5.8 %cholesky.100 = f32[64,64]{1,0:T(8,128)S(1)} custom-call(f32[64,64]{1,0:T(8,128)S(1)} %fusion.81), custom_call_target="Cholesky" | custom-call | tf_op jit(solution)/shard_map/jit(cholesky)/cholesky | solution.py:34
  60.7 4.9 %custom-call.28 = f32[1,64,64]{1,2,0:T(8,128)S(1)} custom-call(f32[1,64,64]{2,1,0:T(8,128)S(1)} %fusion.51), custom_call_target="InvertDiagBlocksLowerTriangular" | custom-call | tf_op jit(solution)/shard_map/triangular_solve | solution.py:36
  67.1 1.8 %collective-permute-start.2 = (f32[192,320]{1,0:T(8,128)S(1)}, f32[192,320]{1,0:T(8,128)S(1)}, u32[]{:S(2)}, u32[]{:S(2)}) collective-permute-start(f32[192,320]{1,0:T(8,128)S(1)} %fusion.6), channel_id=1, source_target_pairs={{0,4},{4,0},{1,5},{5,1},{2,6},{6,2},{3,7},{7,3},{8,12},{12,8},{9,1... | collective-permute-start | bytes 737288 | tf_op jit(solution)/shard_map/ppermute | solution.py:20
  69.0 2.9 %convolution_subtract_fusion = f32[1024,320]{0,1:T(8,128)S(1)} fusion(f32[1024,384]{0,1:T(8,128)} %slice_subtract_fusion, f32[64,320]{1,0:T(8,128)S(1)} %fusion.77, f32[64,320]{1,0:T(8,128)S(1)} %convolution_subtract_fusion.4, pred[]{:T(512)S(6)} %eq.38), kind=kOutput, calls=%fused_computation.5 | convolution fusion | flops 252006400 | bytes 3047425 | tf_op jit(solution)/shard_map/dot_general | solution.py:24
  71.9 3.8 %collective-permute-done.2 = f32[192,320]{1,0:T(8,128)S(1)} collective-permute-done((f32[192,320]{1,0:T(8,128)S(1)}, f32[192,320]{1,0:T(8,128)S(1)}, u32[]{:S(2)}, u32[]{:S(2)}) %collective-permute-start.2) | collective-permute-done | bytes 245792 | tf_op jit(solution)/shard_map/ppermute | solution.py:20
  76.8 5.8 %cholesky.111 = f32[64,64]{1,0:T(8,128)S(1)} custom-call(f32[64,64]{1,0:T(8,128)S(1)} %fusion.76), custom_call_target="Cholesky" | custom-call | tf_op jit(solution)/shard_map/jit(cholesky)/cholesky | solution.py:34
  84.0 4.9 %custom-call.29 = f32[1,64,64]{1,2,0:T(8,128)S(1)} custom-call(f32[1,64,64]{2,1,0:T(8,128)S(1)} %fusion.52), custom_call_target="InvertDiagBlocksLowerTriangular" | custom-call | tf_op jit(solution)/shard_map/triangular_solve | solution.py:36
  91.7 2.0 %convolution_subtract_fusion.1 = f32[1024,256]{0,1:T(8,128)} fusion(f32[1024,320]{0,1:T(8,128)S(1)} %convolution_subtract_fusion, f32[64,256]{1,0:T(8,128)S(1)} %fusion.72, f32[64,256]{1,0:T(8,128)S(1)} %convolution_subtract_fusion.7, pred[]{:T(512)S(6)} %eq.39), kind=kOutput, calls=%fused_computation.6 | convolution fusion | flops 201605120 | bytes 2490369 | tf_op jit(solution)/shard_map/dot_general | solution.py:24
  96.2 5.8 %cholesky.122 = f32[64,64]{1,0:T(8,128)S(1)} custom-call(f32[64,64]{1,0:T(8,128)S(1)} %fusion.71), custom_call_target="Cholesky" | custom-call | tf_op jit(solution)/shard_map/jit(cholesky)/cholesky | solution.py:34
  103.4 4.9 %custom-call.30 = f32[1,64,64]{1,2,0:T(8,128)S(1)} custom-call(f32[1,64,64]{2,1,0:T(8,128)S(1)} %fusion.53), custom_call_target="InvertDiagBlocksLowerTriangular" | custom-call | tf_op jit(solution)/shard_map/triangular_solve | solution.py:36
  109.4 2.6 %collective-permute-start.4 = (f32[64,192]{1,0:T(8,128)S(1)}, f32[64,192]{1,0:T(8,128)S(1)}, u32[]{:S(2)}, u32[]{:S(2)}) collective-permute-start(f32[64,192]{1,0:T(8,128)S(1)} %fusion.33), channel_id=1, source_target_pairs={{0,16},{16,0},{1,17},{17,1},{2,18},{18,2},{3,19},{19,3},{4,20},{20... | collective-permute-start | bytes 147464 | tf_op jit(solution)/shard_map/ppermute | solution.py:20
  112.0 2.0 %convolution_subtract_fusion.2 = f32[1024,192]{0,1:T(8,128)S(1)} fusion(f32[1024,256]{0,1:T(8,128)} %convolution_subtract_fusion.1, f32[64,192]{1,0:T(8,128)S(1)} %fusion.67, f32[64,192]{1,0:T(8,128)S(1)} %convolution_subtract_fusion.6, pred[]{:T(512)S(6)} %eq.40), kind=kOutput, calls=%fused_computation.7 | convolution fusion | flops 151203840 | bytes 1933313 | tf_op jit(solution)/shard_map/dot_general | solution.py:24
  115.7 5.8 %cholesky.133 = f32[64,64]{1,0:T(8,128)S(1)} custom-call(f32[64,64]{1,0:T(8,128)S(1)} %fusion.66), custom_call_target="Cholesky" | custom-call | tf_op jit(solution)/shard_map/jit(cholesky)/cholesky | solution.py:34
  122.8 4.9 %custom-call.31 = f32[1,64,64]{1,2,0:T(8,128)S(1)} custom-call(f32[1,64,64]{2,1,0:T(8,128)S(1)} %fusion.54), custom_call_target="InvertDiagBlocksLowerTriangular" | custom-call | tf_op jit(solution)/shard_map/triangular_solve | solution.py:36
  (89 shorter events, 29.8 us)
Async XLA Ops:
  0.0 12.1 %copy-start = (f32[1024,320]{0,1:T(8,128)S(1)}, f32[1024,320]{0,1:T(8,128)}, u32[]{:S(2)}) copy-start(f32[1024,320]{0,1:T(8,128)} %param.8) | copy-start | bytes 3932164
  2.1 1.5 %copy-start.3 = (f32[1024,128]{0,1:T(8,128)S(1)}, f32[1024,128]{0,1:T(8,128)}, u32[]{:S(2)}) copy-start(f32[1024,128]{0,1:T(8,128)} %copy.6) | copy-start | bytes 1572868
  15.3 2.6 %collective-permute-start = (f32[320,448]{1,0:T(8,128)}, f32[320,448]{1,0:T(8,128)}, u32[]{:S(2)}, u32[]{:S(2)}) collective-permute-start(f32[320,448]{1,0:T(8,128)} %convolution_bitcast_fusion), channel_id=1, source_target_pairs={{0,1},{1,0},{2,3},{3,2},{4,5},{5,4},{6,7},{7,6},{8,9},{9,8},{10,11... | collective-permute-start | bytes 1720328 | tf_op jit(solution)/shard_map/ppermute | solution.py:20
  19.3 0.8 copy-start.4
  19.3 1.4 %copy-start.1 = (f32[320,448]{1,0:T(8,128)}, f32[320,448]{1,0:T(8,128)S(1)}, u32[]{:S(2)}) copy-start(f32[320,448]{1,0:T(8,128)S(1)} %get-tuple-element.6) | copy-start | bytes 1720324
  33.1 3.1 %copy-start.2 = (f32[320,448]{1,0:T(8,128)S(1)}, f32[320,448]{1,0:T(8,128)}, u32[]{:S(2)}) copy-start(f32[320,448]{1,0:T(8,128)} %copy-done.1) | copy-start | bytes 1720324
  38.6 12.6 %collective-permute-start.1 = (f32[256,384]{1,0:T(8,128)}, f32[256,384]{1,0:T(8,128)}, u32[]{:S(2)}, u32[]{:S(2)}) collective-permute-start(f32[256,384]{1,0:T(8,128)} %fusion.5), channel_id=1, source_target_pairs={{0,2},{2,0},{1,3},{3,1},{4,6},{6,4},{5,7},{7,5},{8,10},{10,8},{9,1... | collective-permute-start | bytes 1179656 | tf_op jit(solution)/shard_map/ppermute | solution.py:20
  67.1 8.5 %collective-permute-start.2 = (f32[192,320]{1,0:T(8,128)S(1)}, f32[192,320]{1,0:T(8,128)S(1)}, u32[]{:S(2)}, u32[]{:S(2)}) collective-permute-start(f32[192,320]{1,0:T(8,128)S(1)} %fusion.6), channel_id=1, source_target_pairs={{0,4},{4,0},{1,5},{5,1},{2,6},{6,2},{3,7},{7,3},{8,12},{12,8},{9,1... | collective-permute-start | bytes 737288 | tf_op jit(solution)/shard_map/ppermute | solution.py:20
  90.1 5.0 %collective-permute-start.3 = (f32[128,256]{1,0:T(8,128)S(1)}, f32[128,256]{1,0:T(8,128)S(1)}, u32[]{:S(2)}, u32[]{:S(2)}) collective-permute-start(f32[128,256]{1,0:T(8,128)S(1)} %fusion.12), channel_id=1, source_target_pairs={{0,8},{8,0},{1,9},{9,1},{2,10},{10,2},{3,11},{11,3},{4,12},{12,4},... | collective-permute-start | bytes 393224 | tf_op jit(solution)/shard_map/ppermute | solution.py:20
  109.4 5.2 %collective-permute-start.4 = (f32[64,192]{1,0:T(8,128)S(1)}, f32[64,192]{1,0:T(8,128)S(1)}, u32[]{:S(2)}, u32[]{:S(2)}) collective-permute-start(f32[64,192]{1,0:T(8,128)S(1)} %fusion.33), channel_id=1, source_target_pairs={{0,16},{16,0},{1,17},{17,1},{2,18},{18,2},{3,19},{19,3},{4,20},{20... | collective-permute-start | bytes 147464 | tf_op jit(solution)/shard_map/ppermute | solution.py:20
where the time goes:
time: 130 us
  other arithmetic  64.6 us (50%)
  matrix products  36.2 us (28%)
  waiting for transfers between devices  15 us (12%)
  starting transfers between devices  9.38 us (7%)
  local copies, waits for them, and re-layouts  4.18 us (3%)
    another operation x15, other arithmetic, cholesky_solve(): factor = jnp.linalg.cholesky(block)  32.6 us
    dot_general x39, matrix products, matmul(): jnp.dot(left, right, precision=PRECISE, preferred_element_type=jnp.float32)  30.7 us
    another operation x10, other arithmetic, cholesky_solve(): lax.linalg.triangular_solve(factor, partial_value, left_side=True, lower=...  27.7 us
    ppermute x5, waiting for transfers between devices, swapped(): return lax.ppermute(block, axis, route)  15 us
    ppermute x5, starting transfers between devices, swapped(): return lax.ppermute(block, axis, route)  9.38 us
    dot_general x1, matrix products, inner_rows(): lax.dot_general(left, right, (((0,), (0,)), ((), ())), precision=PRECISE,...  3.14 us
    unnamed x11, local copies, waits for them, and re-layouts  2.81 us
    select_n x5, other arithmetic, body(): lower_gram = jnp.where(is_upper, grams_sib, grams_own)  2.67 us
  transfers between devices with their start and end apart: 5, of which 5 were waited for; matrix products, arithmetic and copies ran while one was open for 7% of the time, Pallas kernels for 0%

commit v1 on v0

v1 whole, which is shorter than its diff:
```python
import functools

import jax
import jax.numpy as jnp
from jax import lax
from jax.experimental import pallas as pl
from jax.experimental.pallas import tpu as pltpu
from jax.sharding import PartitionSpec as P

MESH = pl.DeviceIdType.MESH
CHUNKS = 4


def dot(left, right, dims=((1,), (0,))):
    return lax.dot_general(
        left, right, (dims, ((), ())),
        precision=lax.Precision.HIGHEST, preferred_element_type=jnp.float32,
    )


def halves(value):
    high = value.astype(jnp.bfloat16)
    low = (value - high.astype(jnp.float32)).astype(jnp.bfloat16)
    return high, low


def dot3(left, right, dims=((1,), (0,))):
    def one(a, b):
        return lax.dot_general(a, b, (dims, ((), ())), preferred_element_type=jnp.float32)
    return one(left[0], right[1]) + one(left[1], right[0]) + one(left[0], right[0])


def spd_inverse(block, rank):
    rows = lax.broadcasted_iota(jnp.int32, (rank, rank), 0)
    cols = lax.broadcasted_iota(jnp.int32, (rank, rank), 1)
    eye = jnp.where(rows == cols, 1.0, 0.0).astype(jnp.float32)
    wide = jnp.concatenate([block, eye], 1)
    width = 2 * rank
    tiles = tuple(wide[8 * i:8 * i + 8] for i in range(rank // 8))
    sub = lax.broadcasted_iota(jnp.int32, (8, width), 0)

    def eight(_, tiles):
        tiles = list(tiles)
        for k in range(8):
            row = tiles[0][k:k + 1]
            row = row * (1.0 / row[:, k:k + 1])
            new = [t - t[:, k:k + 1] * row for t in tiles]
            new[0] = jnp.where(sub == k, row, new[0])
            tiles = new
        tiles = [pltpu.roll(t, width - 8, 1) for t in tiles]
        return tuple(tiles[1:] + tiles[:1])

    tiles = lax.fori_loop(0, rank // 8, eight, tiles)
    return jnp.concatenate(tiles, 0)[:, :rank]


def kernel(levels, rank, rhs, leaf, dinv_hbm, u_hbm, v_hbm, r_hbm, out_ref, *scratch):
    (dinv, u, v, r, b_hi, b_lo, x, gram, give, coef_ref, load_sem, send_sem, recv_sem) = scratch[:13]
    tp, tw, rest = scratch[13:13 + levels], scratch[13 + levels:13 + 2 * levels], scratch[13 + 2 * levels:]
    me = lax.axis_index("leaf")
    core = lax.rem(me, 2)
    half = rank // 2

    def flipped(bit):
        return me + (1 - 2 * (me // 2 ** bit % 2)) * 2 ** bit

    def flipped_both(bit):
        return flipped(bit) + 1 - 2 * core

    barrier = pltpu.get_barrier_semaphore()
    friends = [flipped(0)]
    for bit in range(1, levels):
        friends += [flipped(bit), flipped_both(bit)]
    for friend in friends:
        pl.semaphore_signal(barrier, inc=1, device_id=(friend,), device_id_type=MESH)

    step = leaf // CHUNKS
    load_u = pltpu.make_async_copy(u_hbm, u, load_sem.at[0])
    load_r = pltpu.make_async_copy(r_hbm, r, load_sem.at[1])
    load_v = pltpu.make_async_copy(v_hbm, v, load_sem.at[2])
    load_d = [
        pltpu.make_async_copy(
            dinv_hbm.at[pl.ds(i * step, step)], dinv.at[pl.ds(i * step, step)], load_sem.at[3 + i]
        )
        for i in range(CHUNKS)
    ]
    load_u.start()
    load_r.start()
    load_d[0].start()
    load_v.start()
    for load in load_d[1:]:
        load.start()

    load_u.wait()
    load_r.wait()
    for i in range(CHUNKS):
        rows = pl.ds(i * step, step)
        parts = [r[rows]]
        for level in range(levels, 0, -1):
            scale = 2.0 / (leaf * 2.0 ** (level - 1))
            parts.append(u[rows, (level - 1) * rank:level * rank] * scale)
        b_hi[rows], b_lo[rows] = halves(jnp.concatenate(parts, 1))

    for i in range(CHUNKS):
        rows = pl.ds(i * step, step)
        load_d[i].wait()
        if i == 0:
            load_v.wait()
        x_part = dot3(halves(dinv[rows]), (b_hi[...], b_lo[...]))
        x[rows] = x_part
        add = dot3(halves(v[rows]), halves(x_part), ((0,), (0,)))
        gram[...] = add if i == 0 else gram[...] + add

    pl.semaphore_wait(barrier, len(friends))

    rows_i = lax.broadcasted_iota(jnp.int32, (rank, rank), 0)
    cols_i = lax.broadcasted_iota(jnp.int32, (rank, rank), 1)
    eye = jnp.where(rows_i == cols_i, 1.0, 0.0).astype(jnp.float32)

    def send(level, slot, src, dst, target):
        copy = pltpu.make_async_remote_copy(
            src_ref=src, dst_ref=dst,
            send_sem=send_sem.at[level - 1, slot], recv_sem=recv_sem.at[level - 1, slot],
            device_id=(target,), device_id_type=MESH,
        )
        copy.start()
        return copy

    def update_rows(cols):
        keep = cols - rank
        coef = halves(coef_ref[:, :keep])
        for i in range(CHUNKS):
            rows = pl.ds(i * step, step)
            taken = halves(x[rows, keep:cols])
            x[rows, :keep] = x[rows, :keep] - dot3(taken, coef)

    copies = []
    state = None
    cols = rhs + levels * rank
    for level in range(1, levels + 1):
        keep = cols - rank
        bit = me // 2 ** (level - 1) % 2
        p_ref, w_ref = tp[level - 1], tw[level - 1]
        far = flipped(level - 1)
        left = levels - level
        rest_copy = None
        if level == 1:
            p_ref[bit] = gram[:rank, keep:]
            w_ref[bit] = gram[:rank, :keep]
            p_copies = [send(1, 0, p_ref.at[bit], p_ref.at[bit], far)]
            w_copies = [send(1, 3, w_ref.at[bit], w_ref.at[bit], far)]
            for which in range(2):
                for m in range(left):
                    give[which, m * half:(m + 1) * half] = gram[pl.ds((m + 1) * rank + which * half, half)]
            rest_copy = send(1, 6, give.at[1 - core], rest[0].at[bit], far)
            rest[0][bit] = give[core]
        else:
            mine = pl.ds(pl.multiple_of(core * half, half), half)
            p_ref[bit, mine] = state[:half, keep:]
            w_ref[bit, mine] = state[:half, :keep]
            p_copies, w_copies = [], []
            targets = [far, flipped_both(level - 1), flipped(0)]
            for slot, target in enumerate(targets):
                p_copies.append(send(level, slot, p_ref.at[bit, mine], p_ref.at[bit, mine], target))
            for slot, target in enumerate(targets):
                w_copies.append(send(level, 3 + slot, w_ref.at[bit, mine], w_ref.at[bit, mine], target))
            if left:
                rest[level - 1][bit] = state[half:]
                rest_copy = send(level, 6, rest[level - 1].at[bit], rest[level - 1].at[bit], far)
            update_rows(cols + rank)
        copies += p_copies + w_copies
        for copy in p_copies:
            copy.wait_recv()
        across_low, across_up = p_ref[0], p_ref[1]
        schur = eye - dot(across_low, across_up)
        inverse = spd_inverse(dot(schur, schur, ((0,), (0,))), rank)
        solver = dot(inverse, schur, ((1,), (1,)))
        for copy in w_copies:
            copy.wait_recv()
        right_up = w_ref[1]
        high_coef = dot(solver, w_ref[0] - dot(across_low, right_up))
        low_coef = right_up - dot(across_up, high_coef)
        if left:
            copies.append(rest_copy)
            rest_copy.wait_recv()
            rest_ref = rest[level - 1]
            state = (
                (rest_ref[0, :, :keep] - dot(rest_ref[0, :, keep:], low_coef))
                + (rest_ref[1, :, :keep] - dot(rest_ref[1, :, keep:], high_coef))
            )
        coef_ref[:, :keep] = jnp.where(bit == 1, high_coef, low_coef)
        cols = keep

    coef = halves(coef_ref[:, :rhs])
    for i in range(CHUNKS):
        rows = pl.ds(i * step, step)
        out_ref[rows] = x[rows, :rhs] - dot3(halves(x[rows, rhs:rhs + rank]), coef)
    for copy in copies:
        copy.wait_send()


def body(leaf_inverses, u_bases, v_bases, right_side):
    leaf = leaf_inverses.shape[0]
    levels = lax.axis_size("leaf").bit_length() - 1
    rank = u_bases.shape[1] // levels
    rhs = right_side.shape[1]
    cols = rhs + levels * rank
    half = rank // 2
    f32 = jnp.float32
    scratch = [
        pltpu.VMEM(leaf_inverses.shape, f32),
        pltpu.VMEM(u_bases.shape, f32),
        pltpu.VMEM(v_bases.shape, f32),
        pltpu.VMEM(right_side.shape, f32),
        pltpu.VMEM((leaf, cols), jnp.bfloat16),
        pltpu.VMEM((leaf, cols), jnp.bfloat16),
        pltpu.VMEM((leaf, cols), f32),
        pltpu.VMEM((levels * rank, cols), f32),
        pltpu.VMEM((2, (levels - 1) * half, cols), f32),
        pltpu.VMEM((rank, cols - rank), f32),
        pltpu.SemaphoreType.DMA((3 + CHUNKS,)),
        pltpu.SemaphoreType.DMA((levels, 7)),
        pltpu.SemaphoreType.DMA((levels, 7)),
    ]
    widths = [cols - i * rank for i in range(levels)]
    scratch += [pltpu.VMEM((2, rank, rank), f32) for _ in widths]
    scratch += [pltpu.VMEM((2, rank, w - rank), f32) for w in widths]
    scratch += [
        pltpu.VMEM((2, (levels - 1 - i) * half, w), f32) for i, w in enumerate(widths[:-1])
    ]
    return pl.pallas_call(
        functools.partial(kernel, levels, rank, rhs, leaf),
        out_shape=jax.ShapeDtypeStruct(right_side.shape, f32),
        in_specs=[pl.BlockSpec(memory_space=pl.ANY)] * 4,
        out_specs=pl.BlockSpec(memory_space=pltpu.VMEM),
        scratch_shapes=scratch,
        compiler_params=pltpu.CompilerParams(
            collective_id=0, has_side_effects=True, vmem_limit_bytes=48 * 2**20
        ),
        name="tree_solve",
    )(leaf_inverses, u_bases, v_bases, right_side)


def solution(mesh):
    in_specs = (P("leaf", None), P("leaf", None), P("leaf", None), P("leaf", None))
    out_specs = P("leaf", None)
    return jax.shard_map(body, mesh=mesh, in_specs=in_specs, out_specs=out_specs, check_vma=False)
```

time: 130 us -> 68.9 us (0.53)
  other arithmetic: 64.6 us -> 0 us
  Pallas kernels: 0 us -> 63.3 us
  matrix products: 36.2 us -> 0 us
  waiting for transfers between devices: 15 us -> 0 us
  starting transfers between devices: 9.38 us -> 0 us
    pallas_call x0 -> x1, Pallas kernels: none -> 63.3 us  [body(): pl.pallas_call(functools.partial(kernel, levels, rank, rhs, leaf), out_sh...]
    another operation x25 -> x0, other arithmetic: 60.3 us -> none  [the longest x15 32.6 us: cholesky_solve(): factor = jnp.linalg.cholesky(block)]
    dot_general x40 -> x0, matrix products: 33.8 us -> none  [the longest x39 30.7 us: matmul(): jnp.dot(left, right, precision=PRECISE, preferred_element_type=jnp.float32)]
    ppermute x5 -> x0, waiting for transfers between devices: 15 us -> none  [swapped(): return lax.ppermute(block, axis, route)]
    ppermute x5 -> x0, starting transfers between devices: 9.38 us -> none  [swapped(): return lax.ppermute(block, axis, route)]
    select_n x5 -> x0, other arithmetic: 2.67 us -> none  [body(): lower_gram = jnp.where(is_upper, grams_sib, grams_own)]
    unnamed x11 -> x5, local copies, waits for them, and re-layouts: 2.81 us -> 5.4 us
    another operation x10 -> x0, matrix products: 2.36 us -> none  [the longest x5 1.38 us: cholesky_solve(): lax.linalg.triangular_solve(factor, right_cols, left_side=True, lower=True)]
  transfers between devices with their start and end apart: 5 -> 0, of which waited for: 5 -> 0; matrix products, arithmetic and copies ran while one was open for 7% -> 0% of each run, Pallas kernels for 0% -> 0%
where the time goes in v1:
time: 68.9 us; the launch traced here: 68.7 us
  Pallas kernels  63.3 us (92%)
  local copies, waits for them, and re-layouts  5.4 us (8%)
    pallas_call x1, Pallas kernels, body(): pl.pallas_call(functools.partial(kernel, levels, rank, rhs, leaf), out_sh...  63.3 us
    unnamed x5, local copies, waits for them, and re-layouts  5.4 us

profile of v1, /device:TPU:0, one launch (start us, length us, event | category | flops | bytes accessed | tf_op | source)
XLA Modules:
  0.0 68.7 jit_solution(12338513353910418569)
XLA Ops:
  0.0 1.8 %copy.5.u_hbm = f32[1024,320]{1,0:T(8,128)S(1)} copy(f32[1024,320]{0,1:T(8,128)} %param.5) | data formatting | bytes 2621440 | tf_op args[1]
  1.8 1.8 %copy.6.v_hbm = f32[1024,320]{1,0:T(8,128)S(1)} copy(f32[1024,320]{0,1:T(8,128)} %param.6) | data formatting | bytes 2621440 | tf_op args[2]
  3.6 0.0 copy-start
  3.6 1.0 %copy-done = f32[1024,128]{1,0:T(8,128)S(1)} copy-done((f32[1024,128]{1,0:T(8,128)S(1)}, f32[1024,128]{1,0:T(8,128)}, u32[]{:S(2)}) %copy-start) | copy-done | bytes 524312
  4.6 63.3 %tree_solve.1 = f32[1024,128]{1,0:T(8,128)S(1)} custom-call(f32[1024,1024]{1,0:T(8,128)} %dinv_hbm.1, f32[1024,320]{1,0:T(8,128)S(1)} %copy.5.u_hbm, f32[1024,320]{1,0:T(8,128)S(1)} %copy.6.v_hbm, f32[1024,128]{1,0:T(8,128)S(1)} %copy-done), custom_call_target="tpu_custom_call" | custom-call | tf_op jit(solution)/shard_map/tree_solve/pallas_call | solution.py:231
  67.9 0.8 %copy.8 = f32[1024,128]{1,0:T(8,128)} copy(f32[1024,128]{1,0:T(8,128)S(1)} %tree_solve.1) | data formatting | bytes 1048576
Async XLA Ops:
  3.6 1.0 %copy-start = (f32[1024,128]{1,0:T(8,128)S(1)}, f32[1024,128]{1,0:T(8,128)}, u32[]{:S(2)}) copy-start(f32[1024,128]{1,0:T(8,128)} %r_hbm.1) | copy-start | bytes 1572868

commit v2 on v1

v2 whole, which is shorter than its diff:
```python
import functools

import jax
import jax.numpy as jnp
from jax import lax
from jax.experimental import pallas as pl
from jax.experimental.pallas import tpu as pltpu
from jax.sharding import PartitionSpec as P

MESH = pl.DeviceIdType.MESH
CHUNKS = 4


def dot(left, right, dims=((1,), (0,))):
    return lax.dot_general(
        left, right, (dims, ((), ())),
        precision=lax.Precision.HIGHEST, preferred_element_type=jnp.float32,
    )


def halves(value):
    high = value.astype(jnp.bfloat16)
    low = (value - high.astype(jnp.float32)).astype(jnp.bfloat16)
    return high, low


def dot3(left, right, dims=((1,), (0,))):
    def one(a, b):
        return lax.dot_general(a, b, (dims, ((), ())), preferred_element_type=jnp.float32)
    return one(left[0], right[1]) + one(left[1], right[0]) + one(left[0], right[0])


def spd_inverse(block, rank):
    rows = lax.broadcasted_iota(jnp.int32, (rank, rank), 0)
    cols = lax.broadcasted_iota(jnp.int32, (rank, rank), 1)
    eye = jnp.where(rows == cols, 1.0, 0.0).astype(jnp.float32)
    wide = jnp.concatenate([block, eye], 1)
    width = 2 * rank
    tiles = tuple(wide[8 * i:8 * i + 8] for i in range(rank // 8))
    sub = lax.broadcasted_iota(jnp.int32, (8, width), 0)

    def eight(_, tiles):
        tiles = list(tiles)
        for k in range(8):
            row = tiles[0][k:k + 1]
            row = row * (1.0 / row[:, k:k + 1])
            new = [t - t[:, k:k + 1] * row for t in tiles]
            new[0] = jnp.where(sub == k, row, new[0])
            tiles = new
        tiles = [pltpu.roll(t, width - 8, 1) for t in tiles]
        return tuple(tiles[1:] + tiles[:1])

    tiles = lax.fori_loop(0, rank // 8, eight, tiles)
    return jnp.concatenate(tiles, 0)[:, :rank]


def leaf_kernel(levels, rank, rhs, leaf, dinv, u_t, v_t, r, x, gram, b_hi, b_lo):
    index = pl.program_id(0)
    keep = levels * rank

    @pl.when(index == 0)
    def _():
        b_hi[:, :rhs], b_lo[:, :rhs] = halves(r[...])
        parts = []
        for level in range(levels, 0, -1):
            scale = 2.0 / (leaf * 2.0 ** (level - 1))
            parts.append(u_t[(level - 1) * rank:level * rank] * scale)
        b_hi[:, rhs:], b_lo[:, rhs:] = halves(jnp.concatenate(parts, 0).T)
        gram[...] = jnp.zeros_like(gram)

    part = dot3(halves(dinv[...]), (b_hi[...], b_lo[...]))
    x[...] = part
    gram[...] += dot3(halves(v_t[...]), halves(part))


def final_kernel(rhs, x, comp, out):
    out[...] = x[:, :rhs] + dot3(halves(x[:, rhs:]), halves(comp[...]))


def kernel(levels, rank, rhs, gram, comp, *scratch):
    give, send_sem, recv_sem = scratch[:3]
    groups = [scratch[3 + i * levels:3 + (i + 1) * levels] for i in range(4)]
    tp, tw, low_refs, high_refs = groups
    near_refs = scratch[3 + 4 * levels:3 + 4 * levels + levels - 1]
    far_refs = scratch[3 + 4 * levels + levels - 1:]
    me = lax.axis_index("leaf")
    core = lax.rem(me, 2)
    half = rank // 2

    def flipped(bit):
        return me + (1 - 2 * (me // 2 ** bit % 2)) * 2 ** bit

    def flipped_both(bit):
        return flipped(bit) + 1 - 2 * core

    barrier = pltpu.get_barrier_semaphore()
    friends = [flipped(0)]
    for bit in range(1, levels):
        friends += [flipped(bit), flipped_both(bit)]
    for friend in friends:
        pl.semaphore_signal(barrier, inc=1, device_id=(friend,), device_id_type=MESH)
    pl.semaphore_wait(barrier, len(friends))

    rows_i = lax.broadcasted_iota(jnp.int32, (rank, rank), 0)
    cols_i = lax.broadcasted_iota(jnp.int32, (rank, rank), 1)
    eye = jnp.where(rows_i == cols_i, 1.0, 0.0).astype(jnp.float32)

    def send(level, slot, src, dst, target):
        copy = pltpu.make_async_remote_copy(
            src_ref=src, dst_ref=dst,
            send_sem=send_sem.at[level - 1, slot], recv_sem=recv_sem.at[level - 1, slot],
            device_id=(target,), device_id_type=MESH,
        )
        copy.start()
        return copy

    def merged(ref, level, keep):
        return (
            (ref[0, :, :keep] - dot(ref[0, :, keep:], low_refs[level - 1][...]))
            + (ref[1, :, :keep] - dot(ref[1, :, keep:], high_refs[level - 1][...]))
        )

    copies = []
    far_copy = None
    top = None
    cols = rhs + levels * rank
    for level in range(1, levels + 1):
        keep = cols - rank
        bit = me // 2 ** (level - 1) % 2
        p_ref, w_ref = tp[level - 1], tw[level - 1]
        other = flipped(level - 1)
        left = levels - level
        near_copy = None
        next_far = None
        if level == 1:
            p_ref[bit] = gram[:rank, keep:]
            w_ref[bit] = gram[:rank, :keep]
            p_copies = [send(1, 0, p_ref.at[bit], p_ref.at[bit], other)]
            w_copies = [send(1, 3, w_ref.at[bit], w_ref.at[bit], other)]
            for which in range(2):
                for m in range(left):
                    give[which, m * half:(m + 1) * half] = gram[pl.ds((m + 1) * rank + which * half, half)]
            near_copy = send(1, 6, give.at[1 - core, pl.ds(0, half)], near_refs[0].at[bit], other)
            near_refs[0][bit] = give[core, :half]
            if left > 1:
                rows = pl.ds(half, (left - 1) * half)
                next_far = send(1, 7, give.at[1 - core, rows], far_refs[0].at[bit], other)
                far_refs[0][bit] = give[core, half:]
        else:
            mine = pl.ds(pl.multiple_of(core * half, half), half)
            p_ref[bit, mine] = top[:, keep:]
            w_ref[bit, mine] = top[:, :keep]
            p_copies, w_copies = [], []
            targets = [other, flipped_both(level - 1), flipped(0)]
            for slot, target in enumerate(targets):
                p_copies.append(send(level, slot, p_ref.at[bit, mine], p_ref.at[bit, mine], target))
            for slot, target in enumerate(targets):
                w_copies.append(send(level, 3 + slot, w_ref.at[bit, mine], w_ref.at[bit, mine], target))
            if left:
                far_copy.wait_recv()
                state = merged(far_refs[level - 2], level - 1, cols)
                near_ref = near_refs[level - 1]
                near_ref[bit] = state[:half]
                near_copy = send(level, 6, near_ref.at[bit], near_ref.at[bit], other)
                if left > 1:
                    far_ref = far_refs[level - 1]
                    far_ref[bit] = state[half:]
                    next_far = send(level, 7, far_ref.at[bit], far_ref.at[bit], other)
        far_copy = next_far
        copies += p_copies + w_copies + [c for c in (near_copy, next_far) if c is not None]
        for copy in p_copies:
            copy.wait_recv()
        across_low, across_up = p_ref[0], p_ref[1]
        schur = eye - dot(across_low, across_up)
        inverse = spd_inverse(dot(schur, schur, ((0,), (0,))), rank)
        solver = dot(inverse, schur, ((1,), (1,)))
        for copy in w_copies:
            copy.wait_recv()
        right_up = w_ref[1]
        high_coef = dot(solver, w_ref[0] - dot(across_low, right_up))
        low_refs[level - 1][...] = right_up - dot(across_up, high_coef)
        high_refs[level - 1][...] = high_coef
        if left:
            near_copy.wait_recv()
            top = merged(near_refs[level - 1], level, keep)
        cols = keep

    for level in range(levels, 0, -1):
        bit = me // 2 ** (level - 1) % 2
        coef = jnp.where(bit == 1, high_refs[level - 1][...], low_refs[level - 1][...])
        done = (levels - level) * rank
        value = coef[:, :rhs]
        if done:
            value = value + dot(coef[:, rhs:], comp[:done])
        comp[done:done + rank] = -value
    for copy in copies:
        copy.wait_send()


def body(leaf_inverses, u_bases, v_bases, right_side):
    leaf = leaf_inverses.shape[0]
    levels = lax.axis_size("leaf").bit_length() - 1
    rank = u_bases.shape[1] // levels
    rhs = right_side.shape[1]
    inner = levels * rank
    cols = rhs + inner
    half = rank // 2
    step = leaf // CHUNKS
    f32 = jnp.float32
    x, gram = pl.pallas_call(
        functools.partial(leaf_kernel, levels, rank, rhs, leaf),
        grid=(CHUNKS,),
        out_shape=[jax.ShapeDtypeStruct((leaf, cols), f32), jax.ShapeDtypeStruct((inner, cols), f32)],
        in_specs=[
            pl.BlockSpec((step, leaf), lambda i: (i, 0)),
            pl.BlockSpec((inner, leaf), lambda i: (0, 0)),
            pl.BlockSpec((inner, step), lambda i: (0, i)),
            pl.BlockSpec((leaf, rhs), lambda i: (0, 0)),
        ],
        out_specs=[
            pl.BlockSpec((step, cols), lambda i: (i, 0)),
            pl.BlockSpec((inner, cols), lambda i: (0, 0)),
        ],
        scratch_shapes=[pltpu.VMEM((leaf, cols), jnp.bfloat16)] * 2,
        compiler_params=pltpu.CompilerParams(vmem_limit_bytes=40 * 2**20),
        name="leaf_products",
    )(leaf_inverses, u_bases.T, v_bases.T, right_side)

    widths = [cols - i * rank for i in range(levels)]
    scratch = [
        pltpu.VMEM((2, (levels - 1) * half, cols), f32),
        pltpu.SemaphoreType.DMA((levels, 8)),
        pltpu.SemaphoreType.DMA((levels, 8)),
    ]
    scratch += [pltpu.VMEM((2, rank, rank), f32) for _ in widths]
    scratch += [pltpu.VMEM((2, rank, w - rank), f32) for w in widths]
    scratch += [pltpu.VMEM((rank, w - rank), f32) for w in widths] * 2
    scratch += [pltpu.VMEM((2, half, w), f32) for w in widths[:-1]]
    scratch += [
        pltpu.VMEM((2, (levels - 2 - i) * half, w), f32) for i, w in enumerate(widths[:-2])
    ]
    comp = pl.pallas_call(
        functools.partial(kernel, levels, rank, rhs),
        out_shape=jax.ShapeDtypeStruct((inner, rhs), f32),
        in_specs=[pl.BlockSpec(memory_space=pltpu.VMEM)],
        out_specs=pl.BlockSpec(memory_space=pltpu.VMEM),
        scratch_shapes=scratch,
        compiler_params=pltpu.CompilerParams(
            collective_id=0, has_side_effects=True, vmem_limit_bytes=32 * 2**20
        ),
        name="tree_solve",
    )(gram)

    return pl.pallas_call(
        functools.partial(final_kernel, rhs),
        grid=(CHUNKS,),
        out_shape=jax.ShapeDtypeStruct((leaf, rhs), f32),
        in_specs=[
            pl.BlockSpec((step, cols), lambda i: (i, 0)),
            pl.BlockSpec((inner, rhs), lambda i: (0, 0)),
        ],
        out_specs=pl.BlockSpec((step, rhs), lambda i: (i, 0)),
        name="leaf_solution",
    )(x, comp)


def solution(mesh):
    in_specs = (P("leaf", None), P("leaf", None), P("leaf", None), P("leaf", None))
    out_specs = P("leaf", None)
    return jax.shard_map(body, mesh=mesh, in_specs=in_specs, out_specs=out_specs, check_vma=False)
```

time: 68.9 us -> 75.4 us (1.094); the launches traced: 68.7 us -> 74.2 us
  Pallas kernels: 63.3 us -> 66.3 us
  local copies, waits for them, and re-layouts: 5.4 us -> 7.87 us
    pallas_call x1 -> x3, Pallas kernels: 63.3 us -> 66.3 us  [the longest x1 55.8 us: body(): pl.pallas_call(functools.partial(kernel, levels, rank, rhs), out_shape=ja...]
    unnamed x5 -> x12, local copies, waits for them, and re-layouts: 5.4 us -> 7.87 us
where the time goes in v2:
time: 75.4 us; the launch traced here: 74.2 us
  Pallas kernels  66.3 us (88%)
  local copies, waits for them, and re-layouts  7.87 us (10%)
    pallas_call x1, Pallas kernels, body(): pl.pallas_call(functools.partial(kernel, levels, rank, rhs), out_shape=ja...  55.8 us
    unnamed x12, local copies, waits for them, and re-layouts  7.87 us
    pallas_call x1, Pallas kernels, body(): pl.pallas_call(functools.partial(leaf_kernel, levels, rank, rhs, leaf), g...  6.4 us
    pallas_call x1, Pallas kernels, body(): pl.pallas_call(functools.partial(final_kernel, rhs), grid=(CHUNKS,), out_...  4.08 us

profile of v2, /device:TPU:0, one launch (start us, length us, event | category | flops | bytes accessed | tf_op | source)
XLA Modules:
  0.0 74.2 jit_solution(3624490553658694266)
XLA Ops:
  0.0 0.0 copy-start
  0.0 2.2 %copy-done = f32[1024,1024]{1,0:T(8,128)S(1)} copy-done((f32[1024,1024]{1,0:T(8,128)S(1)}, f32[1024,1024]{1,0:T(8,128)}, u32[]{:S(2)}) %copy-start) | copy-done | bytes 4194328
  2.2 0.0 copy-start.2
  2.2 1.3 %copy-done.2 = f32[1024,320]{0,1:T(8,128)S(1)} copy-done((f32[1024,320]{0,1:T(8,128)S(1)}, f32[1024,320]{0,1:T(8,128)}, u32[]{:S(2)}) %copy-start.2) | copy-done | bytes 1310744
  3.5 0.0 copy-start.3
  3.5 1.3 %copy-done.3 = f32[1024,320]{0,1:T(8,128)S(1)} copy-done((f32[1024,320]{0,1:T(8,128)S(1)}, f32[1024,320]{0,1:T(8,128)}, u32[]{:S(2)}) %copy-start.3) | copy-done | bytes 1310744
  4.8 0.0 copy-start.5
  4.8 1.0 %copy-done.5 = f32[1024,128]{1,0:T(8,128)S(1)} copy-done((f32[1024,128]{1,0:T(8,128)S(1)}, f32[1024,128]{1,0:T(8,128)}, u32[]{:S(2)}) %copy-start.5) | copy-done | bytes 524312
  5.9 6.4 %leaf_products.1 = (f32[1024,448]{1,0:T(8,128)S(1)}, f32[320,448]{1,0:T(8,128)S(1)}) custom-call(f32[1024,1024]{1,0:T(8,128)S(1)} %copy-done, f32[320,1024]{1,0:T(8,128)S(1)} %bitcast.2, f32[320,1024]{1,0:T(8,128)S(1)} %bitcast.3, f32[1024,128]{1,0:T(8,128)S(1)} %copy-done.5), custom_call_target="tpu_custom_call" | custom-call | tf_op jit(solution)/shard_map/leaf_products/pallas_call | solution.py:210
  12.3 0.0 copy-start.1
  12.3 1.3 %copy-done.1 = f32[1024,448]{1,0:T(8,128)} copy-done((f32[1024,448]{1,0:T(8,128)}, f32[1024,448]{1,0:T(8,128)S(1)}, u32[]{:S(2)}) %copy-start.1) | copy-done | bytes 1835032
  13.6 55.8 %tree_solve.1.comp = f32[320,128]{1,0:T(8,128)S(1)} custom-call(f32[320,448]{1,0:T(8,128)S(1)} %get-tuple-element.8.gram), custom_call_target="tpu_custom_call" | custom-call | tf_op jit(solution)/shard_map/tree_solve/pallas_call | solution.py:242
  69.5 0.0 copy-start.4
  69.5 0.7 copy-done.4
  70.1 4.1 %leaf_solution.1 = f32[1024,128]{1,0:T(8,128)} custom-call(f32[1024,448]{1,0:T(8,128)} %copy-done.1, f32[320,128]{1,0:T(8,128)} %copy-done.4), custom_call_target="tpu_custom_call" | custom-call | tf_op jit(solution)/shard_map/leaf_solution/pallas_call | solution.py:254
Async XLA Ops:
  0.0 2.2 %copy-start = (f32[1024,1024]{1,0:T(8,128)S(1)}, f32[1024,1024]{1,0:T(8,128)}, u32[]{:S(2)}) copy-start(f32[1024,1024]{1,0:T(8,128)} %dinv.1) | copy-start | bytes 12582916
  2.2 1.3 %copy-start.2 = (f32[1024,320]{0,1:T(8,128)S(1)}, f32[1024,320]{0,1:T(8,128)}, u32[]{:S(2)}) copy-start(f32[1024,320]{0,1:T(8,128)} %param.5) | copy-start | bytes 3932164
  3.5 1.3 %copy-start.3 = (f32[1024,320]{0,1:T(8,128)S(1)}, f32[1024,320]{0,1:T(8,128)}, u32[]{:S(2)}) copy-start(f32[1024,320]{0,1:T(8,128)} %param.6) | copy-start | bytes 3932164
  4.8 1.0 %copy-start.5 = (f32[1024,128]{1,0:T(8,128)S(1)}, f32[1024,128]{1,0:T(8,128)}, u32[]{:S(2)}) copy-start(f32[1024,128]{1,0:T(8,128)} %r.1) | copy-start | bytes 1572868
  12.3 1.4 %copy-start.1 = (f32[1024,448]{1,0:T(8,128)}, f32[1024,448]{1,0:T(8,128)S(1)}, u32[]{:S(2)}) copy-start(f32[1024,448]{1,0:T(8,128)S(1)} %get-tuple-element.7.x) | copy-start | bytes 5505028
  69.5 0.7 copy-start.4
